TPU v7x, 32 devices: a whole 2x2x4 slice. The times are simulated.
32 devices in a mesh: sample: 2 (over y), gz: 4 (over x, core), gy: 4 (over z).
Axes of the slice: x: 2, y: 2, z: 4, core: 2. Of those that a mesh axis runs over, the one named last changes fastest.
Arguments:
- right_side: float32 [64, 64, 256], P(('sample', 'gz'), 'gy'), parts along dimension 0, may hold values from -8 to 8
- labels: int32 [8, 8, 32], P(('sample', 'gz'), 'gy'), parts along dimension 0, may hold values from 0 to 7
- region_coeff: float32 [16], P('sample'), parts along dimension 0, may hold values from 0.2 to 5
- shift_index: int32 [16], P('sample'), parts along dimension 0, may hold values from 0 to 15
- shift_table: float32 [16], replicated, may hold values from 0.1 to 4
- time_step: float32 [2], P('sample'), parts along dimension 0, may hold values from 0.3 to 1
- block_inverse: float32 [8, 128, 128], replicated, as said below
Outputs:
- solution: float32 [8, 64, 64, 256], P(None, ('sample', 'gz'), 'gy'), parts along dimension 1
- residual: float32 [8, 64, 64, 256], P(None, ('sample', 'gz'), 'gy'), parts along dimension 1
There are 2 independent parts, one for each index of `sample`. A program takes and returns all parts, laid end to end along the dimension named above; an argument that names none is the same for every part. Nothing has to cross between parts.
Inputs may be any that keep to these rules, and one draw needn't show every extreme that they name: `shift_index`: a table row for each system. `labels`: a region for each block. `block_inverse`: each block is symmetric and positive definite.
All inputs are finite; a program needn't handle non-finite values.
Results may differ from a plain program's by a relative error of at most 0.00022.
Values sent between devices are 32-bit elements; how exact they have to be, the bound alone decides.
A program may use at most 64 MiB of HBM per device.

v0:
```python
import jax
import jax.numpy as jnp
from jax import lax
from jax.sharding import PartitionSpec as P

SHIFTS = 8
ITERS = 2
BLOCK = 128
NEIGHBOURS = [
    (step_z, step_y, step_x, 0.5 ** (abs(step_z) + abs(step_y) + abs(step_x) - 1))
    for step_z in (-1, 0, 1)
    for step_y in (-1, 0, 1)
    for step_x in (-1, 0, 1)
    if (step_z, step_y, step_x) != (0, 0, 0)
]


def padded_2(block, sides, width):
    for axis, dim in sides:
        count = lax.axis_size(axis)
        forward = [(i, i + 1) for i in range(count - 1)]
        backward = [(target, source) for source, target in forward]
        low = lax.ppermute(
            lax.slice_in_dim(block, block.shape[dim] - width, None, axis=dim), axis, forward
        )
        high = lax.ppermute(lax.slice_in_dim(block, 0, width, axis=dim), axis, backward)
        block = jnp.concatenate([low, block, high], axis=dim)
    return block


def cell_values(labels, region_coeff):
    picked = jnp.where(labels[..., None] == jnp.arange(region_coeff.shape[0]), region_coeff, 0.0)
    table = jnp.sum(picked, axis=-1)
    return jnp.repeat(jnp.repeat(jnp.repeat(table, 8, 0), 8, 1), 8, 2)


def stencil(field, padded, conductivity, padded_cond):
    depth, rows, width = (field.shape[-3], field.shape[-2], field.shape[-1])
    total = jnp.zeros_like(field)
    for step_z, step_y, step_x, weight in NEIGHBOURS:
        beside = padded[
            ...,
            1 + step_z : 1 + step_z + depth,
            1 + step_y : 1 + step_y + rows,
            1 + step_x : 1 + step_x + width,
        ]
        cond_beside = padded_cond[
            1 + step_z : 1 + step_z + depth,
            1 + step_y : 1 + step_y + rows,
            1 + step_x : 1 + step_x + width,
        ]
        total = total + weight * 0.5 * (conductivity + cond_beside) * (field - beside)
    return total


def extend_field(field):
    extended = padded_2(field, (("gz", 1), ("gy", 2)), 1)
    return jnp.pad(extended, ((0, 0), (0, 0), (0, 0), (1, 1)))


def global_sum(values):
    row_sum = lax.psum(values, "gy")
    return lax.psum(row_sum, "gz")


def precondition(residual, block_inverse):
    shape = residual.shape
    blocks = residual.reshape(shape[0], shape[1], shape[2], shape[3] // BLOCK, BLOCK)
    result = jnp.einsum("szyxb,sbc->szyxc", blocks, block_inverse, precision=lax.Precision.HIGHEST)
    return result.reshape(shape)


def per_system(values):
    return values.reshape(values.shape[0], 1, 1, 1)


def on_device(right_side, labels, region_coeff, shift_index, shift_table, time_step, block_inverse):
    conductivity = cell_values(labels, region_coeff)
    cond_rim = padded_2(conductivity, (("gz", 0), ("gy", 1)), 1)
    padded_cond = jnp.pad(cond_rim, ((0, 0), (0, 0), (1, 1)))
    shift_values = jnp.sum(
        jnp.where(shift_index[:, None] == jnp.arange(shift_table.shape[0]), shift_table, 0.0),
        axis=1,
    )
    scale = time_step[0]
    residual = jnp.broadcast_to(right_side[None], (SHIFTS,) + right_side.shape)
    solution = jnp.zeros_like(residual)
    precond = precondition(residual, block_inverse)
    direction = precond
    rz_now = global_sum(jnp.sum(residual * precond, axis=(1, 2, 3)))
    for iteration in range(ITERS):
        padded = extend_field(direction)
        image = per_system(shift_values) * direction + scale * stencil(
            direction, padded, conductivity, padded_cond
        )
        curvature = global_sum(jnp.sum(direction * image, axis=(1, 2, 3)))
        alpha = per_system(rz_now / curvature)
        solution = solution + alpha * direction
        residual = residual - alpha * image
        precond = precondition(residual, block_inverse)
        rz_next = global_sum(jnp.sum(residual * precond, axis=(1, 2, 3)))
        direction = precond + per_system(rz_next / rz_now) * direction
        rz_now = rz_next
    return (solution, residual)


def solution(mesh):
    in_specs = (
        P(("sample", "gz"), "gy", None),
        P(("sample", "gz"), "gy", None),
        P("sample"),
        P("sample"),
        P(),
        P("sample"),
        P(),
    )
    out_specs = (P(None, ("sample", "gz"), "gy", None), P(None, ("sample", "gz"), "gy", None))
    return jax.shard_map(
        on_device, mesh=mesh, in_specs=in_specs, out_specs=out_specs, check_vma=False
    )
```

profile of v0, /device:TPU:0, one launch (start us, length us, event | category | flops | bytes accessed | tf_op | source)
XLA Modules:
  0.0 131.5 jit_solution(17609959154963669425)
XLA Ops:
  0.6 0.0 copy-start
  0.6 0.0 copy-start.11
  0.7 0.8 select_reduce_fusion
  1.5 0.1 copy.32
  1.6 1.3 collective-permute-start.1
  2.9 3.0 %collective-permute-start = (f32[1,16,256]{1,2,0:T(8,128)S(1)}, f32[1,16,256]{1,2,0:T(8,128)S(1)}, u32[]{:S(2)}, u32[]{:S(2)}) collective-permute-start(f32[1,16,256]{1,2,0:T(8,128)S(1)} %get-tuple-element.54), channel_id=1, source_target_pairs={{0,4},{4,8},{8,12},{1,5},{5,9},{9,13},{2,6},{6,10},{10,14},{3,7},{... | collective-permute-start | bytes 49160 | tf_op jit(solution)/shard_map/ppermute | solution.py:23
  6.0 0.9 copy_bitcast_fusion.1
  6.9 1.1 multiply_reduce_fusion.2
  8.0 0.1 copy_bitcast_fusion
  8.0 0.0 copy-start.4
  8.0 1.0 copy-done.4
  9.0 1.3 collective-permute-start.5
  10.3 5.1 %collective-permute-start.4 = (f32[8,1,16,256]{3,2,1,0:T(8,128)S(1)}, f32[8,1,16,256]{3,2,1,0:T(8,128)S(1)}, u32[]{:S(2)}, u32[]{:S(2)}) collective-permute-start(f32[8,1,16,256]{3,2,1,0:T(8,128)S(1)} %get-tuple-element.19), channel_id=1, source_target_pairs={{0,4},{4,8},{8,12},{1,5},{5,9},{9,13},{2,6},{6,10},{10,14},{3,7},{... | collective-permute-start | bytes 393224 | tf_op jit(solution)/shard_map/ppermute | solution.py:23
  15.5 0.2 select_reduce_fusion.1
  16.3 0.1 copy.33
  16.4 0.0 collective-permute-done.1
  16.4 0.1 copy.35
  16.5 0.0 collective-permute-done
  16.5 0.1 copy.34
  16.6 3.5 %collective-permute-start.2 = (f32[10,1,256]{2,1,0:T(1,128)S(1)}, f32[10,1,256]{2,1,0:T(1,128)S(1)}, u32[]{:S(2)}, u32[]{:S(2)}) collective-permute-start(f32[10,1,256]{2,1,0:T(1,128)S(1)} %get-tuple-element.46), channel_id=1, source_target_pairs={{0,1},{1,2},{2,3},{4,5},{5,6},{6,7},{8,9},{9,10},{10,11},{12,13},{... | collective-permute-start | bytes 30728 | tf_op jit(solution)/shard_map/ppermute | solution.py:23
  20.1 1.3 collective-permute-start.3
  21.4 0.8 fusion.153
  22.1 0.0 collective-permute-done.2
  22.1 3.5 %collective-permute-done.3 = f32[10,1,256]{2,1,0:T(1,128)S(1)} collective-permute-done((f32[10,1,256]{2,1,0:T(1,128)S(1)}, f32[10,1,256]{2,1,0:T(1,128)S(1)}, u32[]{:S(2)}, u32[]{:S(2)}) %collective-permute-start.3) | collective-permute-done | bytes 10272 | tf_op jit(solution)/shard_map/ppermute | solution.py:26
  25.6 0.2 select_maximum_fusion.6
  25.9 1.5 %fusion.157 = (f32[8,16,256]{2,1,0:T(8,128)S(1)}, f32[8,16,256]{2,1,0:T(8,128)S(1)}, f32[8,16,256]{2,1,0:T(8,128)S(1)}, f32[8,16,256]{2,1,0:T(8,128)S(1)}, f32[8...) fusion(f32[10,18,258]{2,1,0:T(8,128)S(1)} %select_maximum_fusio, ...), kind=kLoop, calls=%fused_computation.268 | loop fusion | flops 1179648 | bytes 4734976 | tf_op jit(solution)/shard_map/mul | solution.py:52
  27.4 0.0 collective-permute-done.4
  27.5 0.1 constant_dynamic-update-slice_fusion.1
  27.6 0.0 collective-permute-done.5
  27.6 0.0 copy-start.8
  27.6 0.1 fusion.160
  27.7 3.5 %collective-permute-start.6 = (f32[8,10,1,256]{3,2,1,0:T(1,128)S(1)}, f32[8,10,1,256]{3,2,1,0:T(1,128)S(1)}, u32[]{:S(2)}, u32[]{:S(2)}) collective-permute-start(f32[8,10,1,256]{3,2,1,0:T(1,128)S(1)} %get-tuple-element.14), channel_id=1, source_target_pairs={{0,1},{1,2},{2,3},{4,5},{5,6},{6,7},{8,9},{9,10},{10,11},{12,13},{... | collective-permute-start | bytes 245768 | tf_op jit(solution)/shard_map/ppermute | solution.py:23
  31.2 1.3 collective-permute-start.7
  32.5 0.9 fusion.156
  33.4 0.0 collective-permute-done.6
  33.4 4.1 %collective-permute-done.7 = f32[8,10,1,256]{3,2,1,0:T(1,128)S(1)} collective-permute-done((f32[8,10,1,256]{3,2,1,0:T(1,128)S(1)}, f32[8,10,1,256]{3,2,1,0:T(1,128)S(1)}, u32[]{:S(2)}, u32[]{:S(2)}) %collective-permute-start.7) | collective-permute-done | bytes 81952 | tf_op jit(solution)/shard_map/ppermute | solution.py:26
  37.6 1.5 %select_maximum_fusion.4 = f32[8,10,18,258]{3,2,1,0:T(8,128)S(1)} fusion(f32[8,10,1,256]{3,2,1,0:T(1,128)S(1)} %collective-permute-done.7, f32[8,10,16,256]{3,2,1,0:T(8,128)S(1)} %constant_dynamic-update-slice_fusion, f32[8,10,1,256]{3,2,1,0:T(1,128)S(1)} %collective-permute-done.6), kind=kLoop, calls=%fused_computation.6 | loop fusion | flops 2972160 | bytes 2960640 | tf_op jit(solution)/shard_map/concatenate | solution.py:27
  39.1 0.0 copy-start.5
  39.1 9.8 %multiply_reduce_fusion.1 = (f32[8]{0:T(128)S(1)}, f32[8,8,16,256]{3,2,1,0:T(8,128)S(1)}) fusion(f32[8,8,16,256]{3,2,1,0:T(8,128)} %copy-done.4, f32[8,10,18,258]{3,2,1,0:T(8,128)S(1)} %select_maximum_fusion.4, f32[8,16,256]{2,1,0:T(8,128)} %get-tuple-element.37, f32[8,10,1,256]{3,2,1,0:T(1,128)} %copy-done.10, f32[8,10,16,256]{3,2,1,0:T(8,128)} %copy-done.3, ...), kind=kLoop, calls=%fused_computation.198 | loop fusion | flops 23592952 | bytes 27164740 | tf_op jit(solution)/shard_map/reduce_sum | solution.py:96
  49.0 0.0 copy-start.1
  49.0 9.9 %all-reduce.3 = (f32[8]{0:T(128)S(1)}, f32[8]{0:T(128)S(1)}) all-reduce(f32[8]{0:T(128)S(1)} %get-tuple-element.57, f32[8]{0:T(128)S(1)} %get-tuple-element.8), channel_id=1, replica_groups=mesh['sample'=2,'gz'=4,'gy'=4] {'gy'}, use_global_device_ids=true, to_apply=%region_1.2 | all-reduce | flops 16 | bytes 128 | tf_op jit(solution)/shard_map/psum | solution.py:62
  58.9 5.6 %all-reduce.4 = (f32[8]{0:T(128)S(1)}, f32[8]{0:T(128)S(1)}) all-reduce(f32[8]{0:T(128)S(1)} %get-tuple-element.2, f32[8]{0:T(128)S(1)} %get-tuple-element.3), channel_id=1, replica_groups=mesh['sample'=2,'gz'=4,'gy'=4] {'gz'}, use_global_device_ids=true, to_apply=%region_2.3 | all-reduce | flops 16 | bytes 128 | tf_op jit(solution)/shard_map/psum | solution.py:63
  64.6 1.2 convolution_bitcast_fusion
  65.8 0.0 copy-start.2
  65.8 1.0 copy-done.2
  66.7 0.3 fusion.40
  67.1 8.8 %psum.60 = f32[8]{0:T(128)S(1)} all-reduce(f32[8]{0:T(128)S(1)} %fusion.40), channel_id=1, replica_groups=mesh['sample'=2,'gz'=4,'gy'=4] {'gy'}, use_global_device_ids=true, to_apply=%region_9.10 | all-reduce | flops 8 | bytes 64 | tf_op jit(solution)/shard_map/psum | solution.py:62
  75.8 5.6 %psum.61 = f32[8]{0:T(128)S(1)} all-reduce(f32[8]{0:T(128)S(1)} %psum.60), channel_id=1, replica_groups=mesh['sample'=2,'gz'=4,'gy'=4] {'gz'}, use_global_device_ids=true, to_apply=%region_10.11 | all-reduce | flops 8 | bytes 64 | tf_op jit(solution)/shard_map/psum | solution.py:63
  81.5 1.5 %bitcast_add_fusion = f32[8,8,16,256]{3,2,1,0:T(8,128)S(1)} fusion(f32[8,8,2,2,8,128]{5,4,3,2,1,0:T(8,128)} %copy-done.2, f32[8]{0:T(128)S(1)} %div.10, f32[8,8,16,2,128]{4,2,3,1,0:T(8,128)S(1)} %get-tuple-element.58), kind=kLoop, calls=%fused_computation.59 | loop fusion | flops 524288 | bytes 3145760 | tf_op jit(solution)/shard_map/add | solution.py:102
  83.1 1.9 %collective-permute-start.8 = (f32[8,1,16,256]{3,2,1,0:T(8,128)S(1)}, f32[8,1,16,256]{3,2,1,0:T(8,128)S(1)}, u32[]{:S(2)}, u32[]{:S(2)}) collective-permute-start(f32[8,1,16,256]{3,2,1,0:T(8,128)S(1)} %get-tuple-element.16), channel_id=1, source_target_pairs={{0,4},{4,8},{8,12},{1,5},{5,9},{9,13},{2,6},{6,10},{10,14},{3,7},{... | collective-permute-start | bytes 393224 | tf_op jit(solution)/shard_map/ppermute | solution.py:23
  85.0 1.3 collective-permute-start.9
  86.3 0.0 collective-permute-done.8
  86.3 3.4 %collective-permute-done.9 = f32[8,1,16,256]{3,2,1,0:T(8,128)S(1)} collective-permute-done((f32[8,1,16,256]{3,2,1,0:T(8,128)S(1)}, f32[8,1,16,256]{3,2,1,0:T(8,128)S(1)}, u32[]{:S(2)}, u32[]{:S(2)}) %collective-permute-start.9) | collective-permute-done | bytes 131104 | tf_op jit(solution)/shard_map/ppermute | solution.py:26
  89.7 0.1 pad_maximum_fusion.12
  89.8 3.5 %collective-permute-start.10 = (f32[8,10,1,256]{3,2,1,0:T(1,128)S(1)}, f32[8,10,1,256]{3,2,1,0:T(1,128)S(1)}, u32[]{:S(2)}, u32[]{:S(2)}) collective-permute-start(f32[8,10,1,256]{3,2,1,0:T(1,128)S(1)} %get-tuple-element.12), channel_id=1, source_target_pairs={{0,1},{1,2},{2,3},{4,5},{5,6},{6,7},{8,9},{9,10},{10,11},{12,13},{... | collective-permute-start | bytes 245768 | tf_op jit(solution)/shard_map/ppermute | solution.py:23
  93.3 1.5 %collective-permute-start.11 = (f32[8,10,1,256]{3,2,1,0:T(1,128)S(1)}, f32[8,10,1,256]{3,2,1,0:T(1,128)S(1)}, u32[]{:S(2)}, u32[]{:S(2)}) collective-permute-start(f32[8,10,1,256]{3,2,1,0:T(1,128)S(1)} %get-tuple-element.13), channel_id=1, source_target_pairs={{1,0},{2,1},{3,2},{5,4},{6,5},{7,6},{9,8},{10,9},{11,10},{13,12},{... | collective-permute-start | bytes 245768 | tf_op jit(solution)/shard_map/ppermute | solution.py:26
  94.8 0.6 collective-permute-done.10
  95.3 4.3 %collective-permute-done.11 = f32[8,10,1,256]{3,2,1,0:T(1,128)S(1)} collective-permute-done((f32[8,10,1,256]{3,2,1,0:T(1,128)S(1)}, f32[8,10,1,256]{3,2,1,0:T(1,128)S(1)}, u32[]{:S(2)}, u32[]{:S(2)}) %collective-permute-start.11) | collective-permute-done | bytes 81952 | tf_op jit(solution)/shard_map/ppermute | solution.py:26
  99.6 1.5 %select_maximum_fusion = f32[8,10,18,258]{3,2,1,0:T(8,128)S(1)} fusion(f32[8,10,1,256]{3,2,1,0:T(1,128)S(1)} %collective-permute-done.11, f32[8,10,1,256]{3,2,1,0:T(1,128)S(1)} %collective-permute-done.10, f32[8,1,16,256]{3,2,1,0:T(8,128)S(1)} %collective-permute-done.9, f32[8,8,16,256]{3,2,1,0:T(8,128)S(1)} %bitcast_add_fusion, ...), kind=kLoop, calls=%fused_computation.2 | loop fusion | flops 4458240 | bytes 2960640 | tf_op jit(solution)/shard_map/concatenate | solution.py:27
  101.1 2.4 %maximum_maximum_fusion = (f32[8,10,17,256]{3,2,1,0:T(8,128)}, f32[8,10,17,256]{3,2,1,0:T(8,128)}) fusion(f32[8,1,16,256]{3,2,1,0:T(8,128)S(1)} %collective-permute-done.9, f32[8,8,16,256]{3,2,1,0:T(8,128)S(1)} %bitcast_add_fusion, f32[8,1,16,256]{3,2,1,0:T(8,128)S(1)} %collective-permute-done.8, f32[8,10,1,256]{3,2,1,0:T(1,128)S(1)} %collective-permute-done.10, ...), kind=kLoop, calls=%fused_computation.17 | loop fusion | flops 2088960 | bytes 4259840 | tf_op jit(solution)/shard_map/concatenate | solution.py:27
  103.5 9.4 %multiply_reduce_fusion = (f32[8]{0:T(128)S(1)}, f32[8,8,16,256]{3,2,1,0:T(8,128)}) fusion(f32[8,8,16,256]{3,2,1,0:T(8,128)S(1)} %bitcast_add_fusion, f32[8,10,18,258]{3,2,1,0:T(8,128)S(1)} %select_maximum_fusion, f32[8,16,256]{2,1,0:T(8,128)} %get-tuple-element.37, f32[8,10,17,256]{3,2,1,0:T(8,128)} %get-tuple-element.11, ...), kind=kLoop, calls=%fused_computation.196 | loop fusion | flops 22020088 | bytes 30933060 | tf_op jit(solution)/shard_map/reduce_sum | solution.py:96
  112.9 8.4 %psum.62 = f32[8]{0:T(128)S(1)} all-reduce(f32[8]{0:T(128)S(1)} %get-tuple-element.6), channel_id=1, replica_groups=mesh['sample'=2,'gz'=4,'gy'=4] {'gy'}, use_global_device_ids=true, to_apply=%region_12.13 | all-reduce | flops 8 | bytes 64 | tf_op jit(solution)/shard_map/psum | solution.py:62
  121.3 6.8 %psum.63 = f32[8]{0:T(128)S(1)} all-reduce(f32[8]{0:T(128)S(1)} %psum.62), channel_id=1, replica_groups=mesh['sample'=2,'gz'=4,'gy'=4] {'gz'}, use_global_device_ids=true, to_apply=%region_13.14 | all-reduce | flops 8 | bytes 64 | tf_op jit(solution)/shard_map/psum | solution.py:63
  128.1 3.4 %multiply_subtract_fusion = (f32[8,8,16,256]{3,2,1,0:T(8,128)}, f32[8,8,16,256]{3,2,1,0:T(8,128)}) fusion(f32[8,8,16,256]{3,2,1,0:T(8,128)} %get-tuple-element.7, f32[8,8,16,256]{3,2,1,0:T(8,128)} %copy-done.1, f32[8]{0:T(128)S(1)} %div.11, f32[8,16,256]{2,1,0:T(8,128)S(1)} %copy-done.5, f32[8]{0:T(128)S(1)} %div.9, ...), kind=kLoop, calls=%fused_computation.194 | loop fusion | flops 1835008 | bytes 6422592 | tf_op jit(solution)/shard_map/sub | solution.py:99
  (29 shorter events, 0.2 us)
Async XLA Ops:
  0.6 6.2 %copy-start = (f32[8,128,128]{2,1,0:T(8,128)S(1)}, f32[8,128,128]{2,1,0:T(8,128)}, u32[]{:S(2)}) copy-start(f32[8,128,128]{2,1,0:T(8,128)} %param.13) | copy-start | bytes 1572868
  0.6 14.8 %copy-start.11 = (f32[16]{0:T(128)S(1)}, f32[16]{0:T(128)}, u32[]{:S(2)}) copy-start(f32[16]{0:T(128)} %param.11) | copy-start | bytes 196
  0.7 14.8 %copy-start.12 = (s32[8]{0:T(128)S(1)}, s32[8]{0:T(128)}, u32[]{:S(2)}) copy-start(s32[8]{0:T(128)} %param.10) | copy-start | bytes 100
  1.6 14.8 %collective-permute-start.1 = (f32[1,16,256]{1,2,0:T(8,128)S(1)}, f32[1,16,256]{1,2,0:T(8,128)S(1)}, u32[]{:S(2)}, u32[]{:S(2)}) collective-permute-start(f32[1,16,256]{1,2,0:T(8,128)S(1)} %get-tuple-element.54), channel_id=1, source_target_pairs={{4,0},{8,4},{12,8},{5,1},{9,5},{13,9},{6,2},{10,6},{14,10},{7,3},{... | collective-permute-start | bytes 49160 | tf_op jit(solution)/shard_map/ppermute | solution.py:26
  2.9 13.6 %collective-permute-start = (f32[1,16,256]{1,2,0:T(8,128)S(1)}, f32[1,16,256]{1,2,0:T(8,128)S(1)}, u32[]{:S(2)}, u32[]{:S(2)}) collective-permute-start(f32[1,16,256]{1,2,0:T(8,128)S(1)} %get-tuple-element.54), channel_id=1, source_target_pairs={{0,4},{4,8},{8,12},{1,5},{5,9},{9,13},{2,6},{6,10},{10,14},{3,7},{... | collective-permute-start | bytes 49160 | tf_op jit(solution)/shard_map/ppermute | solution.py:23
  8.0 1.0 copy-start.4
  9.0 18.5 %collective-permute-start.5 = (f32[8,1,16,256]{3,2,1,0:T(8,128)S(1)}, f32[8,1,16,256]{3,2,1,0:T(8,128)S(1)}, u32[]{:S(2)}, u32[]{:S(2)}) collective-permute-start(f32[8,1,16,256]{3,2,1,0:T(8,128)S(1)} %get-tuple-element.18), channel_id=1, source_target_pairs={{4,0},{8,4},{12,8},{5,1},{9,5},{13,9},{6,2},{10,6},{14,10},{7,3},{... | collective-permute-start | bytes 393224 | tf_op jit(solution)/shard_map/ppermute | solution.py:26
  10.3 17.1 %collective-permute-start.4 = (f32[8,1,16,256]{3,2,1,0:T(8,128)S(1)}, f32[8,1,16,256]{3,2,1,0:T(8,128)S(1)}, u32[]{:S(2)}, u32[]{:S(2)}) collective-permute-start(f32[8,1,16,256]{3,2,1,0:T(8,128)S(1)} %get-tuple-element.19), channel_id=1, source_target_pairs={{0,4},{4,8},{8,12},{1,5},{5,9},{9,13},{2,6},{6,10},{10,14},{3,7},{... | collective-permute-start | bytes 393224 | tf_op jit(solution)/shard_map/ppermute | solution.py:23
  16.6 5.5 %collective-permute-start.2 = (f32[10,1,256]{2,1,0:T(1,128)S(1)}, f32[10,1,256]{2,1,0:T(1,128)S(1)}, u32[]{:S(2)}, u32[]{:S(2)}) collective-permute-start(f32[10,1,256]{2,1,0:T(1,128)S(1)} %get-tuple-element.46), channel_id=1, source_target_pairs={{0,1},{1,2},{2,3},{4,5},{5,6},{6,7},{8,9},{9,10},{10,11},{12,13},{... | collective-permute-start | bytes 30728 | tf_op jit(solution)/shard_map/ppermute | solution.py:23
  20.1 5.6 %collective-permute-start.3 = (f32[10,1,256]{2,1,0:T(1,128)S(1)}, f32[10,1,256]{2,1,0:T(1,128)S(1)}, u32[]{:S(2)}, u32[]{:S(2)}) collective-permute-start(f32[10,1,256]{2,1,0:T(1,128)S(1)} %get-tuple-element.47), channel_id=1, source_target_pairs={{1,0},{2,1},{3,2},{5,4},{6,5},{7,6},{9,8},{10,9},{11,10},{13,12},{... | collective-permute-start | bytes 30728 | tf_op jit(solution)/shard_map/ppermute | solution.py:26
  27.4 11.7 %copy-start.6 = (f32[8,16,256]{2,1,0:T(8,128)}, f32[8,16,256]{2,1,0:T(8,128)S(1)}, u32[]{:S(2)}) copy-start(f32[8,16,256]{2,1,0:T(8,128)S(1)} %get-tuple-element.25) | copy-start | bytes 393220
  27.4 11.7 %copy-start.7 = (f32[8,16,256]{2,1,0:T(8,128)}, f32[8,16,256]{2,1,0:T(8,128)S(1)}, u32[]{:S(2)}) copy-start(f32[8,16,256]{2,1,0:T(8,128)S(1)} %get-tuple-element.26) | copy-start | bytes 393220
  27.4 11.6 %copy-start.9 = (f32[8,1,16,256]{3,2,1,0:T(8,128)}, f32[8,1,16,256]{3,2,1,0:T(8,128)S(1)}, u32[]{:S(2)}) copy-start(f32[8,1,16,256]{3,2,1,0:T(8,128)S(1)} %collective-permute-done.4) | copy-start | bytes 393220
  27.6 11.5 %copy-start.8 = (f32[8,1,16,256]{3,2,1,0:T(8,128)}, f32[8,1,16,256]{3,2,1,0:T(8,128)S(1)}, u32[]{:S(2)}) copy-start(f32[8,1,16,256]{3,2,1,0:T(8,128)S(1)} %collective-permute-done.5) | copy-start | bytes 393220
  27.6 11.5 %copy-start.3 = (f32[8,10,16,256]{3,2,1,0:T(8,128)}, f32[8,10,16,256]{3,2,1,0:T(8,128)S(1)}, u32[]{:S(2)}) copy-start(f32[8,10,16,256]{3,2,1,0:T(8,128)S(1)} %constant_dynamic-update-slice_fusion) | copy-start | bytes 3932164
  27.7 5.7 %collective-permute-start.6 = (f32[8,10,1,256]{3,2,1,0:T(1,128)S(1)}, f32[8,10,1,256]{3,2,1,0:T(1,128)S(1)}, u32[]{:S(2)}, u32[]{:S(2)}) collective-permute-start(f32[8,10,1,256]{3,2,1,0:T(1,128)S(1)} %get-tuple-element.14), channel_id=1, source_target_pairs={{0,1},{1,2},{2,3},{4,5},{5,6},{6,7},{8,9},{9,10},{10,11},{12,13},{... | collective-permute-start | bytes 245768 | tf_op jit(solution)/shard_map/ppermute | solution.py:23
  31.2 6.3 %collective-permute-start.7 = (f32[8,10,1,256]{3,2,1,0:T(1,128)S(1)}, f32[8,10,1,256]{3,2,1,0:T(1,128)S(1)}, u32[]{:S(2)}, u32[]{:S(2)}) collective-permute-start(f32[8,10,1,256]{3,2,1,0:T(1,128)S(1)} %get-tuple-element.15), channel_id=1, source_target_pairs={{1,0},{2,1},{3,2},{5,4},{6,5},{7,6},{9,8},{10,9},{11,10},{13,12},{... | collective-permute-start | bytes 245768 | tf_op jit(solution)/shard_map/ppermute | solution.py:26
  37.6 1.5 %copy-start.10 = (f32[8,10,1,256]{3,2,1,0:T(1,128)}, f32[8,10,1,256]{3,2,1,0:T(1,128)S(1)}, u32[]{:S(2)}) copy-start(f32[8,10,1,256]{3,2,1,0:T(1,128)S(1)} %collective-permute-done.7) | copy-start | bytes 245764
  39.1 25.4 %copy-start.5 = (f32[8,16,256]{2,1,0:T(8,128)S(1)}, f32[8,16,256]{2,1,0:T(8,128)}, u32[]{:S(2)}) copy-start(f32[8,16,256]{2,1,0:T(8,128)} %param.7) | copy-start | bytes 393220
  49.0 32.5 %copy-start.1 = (f32[8,8,16,256]{3,2,1,0:T(8,128)}, f32[8,8,16,256]{3,2,1,0:T(8,128)S(1)}, u32[]{:S(2)}) copy-start(f32[8,8,16,256]{3,2,1,0:T(8,128)S(1)} %get-tuple-element.9) | copy-start | bytes 3145732
  65.8 1.0 copy-start.2
  83.1 3.2 %collective-permute-start.8 = (f32[8,1,16,256]{3,2,1,0:T(8,128)S(1)}, f32[8,1,16,256]{3,2,1,0:T(8,128)S(1)}, u32[]{:S(2)}, u32[]{:S(2)}) collective-permute-start(f32[8,1,16,256]{3,2,1,0:T(8,128)S(1)} %get-tuple-element.16), channel_id=1, source_target_pairs={{0,4},{4,8},{8,12},{1,5},{5,9},{9,13},{2,6},{6,10},{10,14},{3,7},{... | collective-permute-start | bytes 393224 | tf_op jit(solution)/shard_map/ppermute | solution.py:23
  85.0 4.7 %collective-permute-start.9 = (f32[8,1,16,256]{3,2,1,0:T(8,128)S(1)}, f32[8,1,16,256]{3,2,1,0:T(8,128)S(1)}, u32[]{:S(2)}, u32[]{:S(2)}) collective-permute-start(f32[8,1,16,256]{3,2,1,0:T(8,128)S(1)} %get-tuple-element.17), channel_id=1, source_target_pairs={{4,0},{8,4},{12,8},{5,1},{9,5},{13,9},{6,2},{10,6},{14,10},{7,3},{... | collective-permute-start | bytes 393224 | tf_op jit(solution)/shard_map/ppermute | solution.py:26
  89.8 5.5 %collective-permute-start.10 = (f32[8,10,1,256]{3,2,1,0:T(1,128)S(1)}, f32[8,10,1,256]{3,2,1,0:T(1,128)S(1)}, u32[]{:S(2)}, u32[]{:S(2)}) collective-permute-start(f32[8,10,1,256]{3,2,1,0:T(1,128)S(1)} %get-tuple-element.12), channel_id=1, source_target_pairs={{0,1},{1,2},{2,3},{4,5},{5,6},{6,7},{8,9},{9,10},{10,11},{12,13},{... | collective-permute-start | bytes 245768 | tf_op jit(solution)/shard_map/ppermute | solution.py:23
  93.3 6.3 %collective-permute-start.11 = (f32[8,10,1,256]{3,2,1,0:T(1,128)S(1)}, f32[8,10,1,256]{3,2,1,0:T(1,128)S(1)}, u32[]{:S(2)}, u32[]{:S(2)}) collective-permute-start(f32[8,10,1,256]{3,2,1,0:T(1,128)S(1)} %get-tuple-element.13), channel_id=1, source_target_pairs={{1,0},{2,1},{3,2},{5,4},{6,5},{7,6},{9,8},{10,9},{11,10},{13,12},{... | collective-permute-start | bytes 245768 | tf_op jit(solution)/shard_map/ppermute | solution.py:26
where the time goes:
time: 132 us
  blocking collectives  45.2 us (34%)
  other arithmetic  34.4 us (26%)
  starting transfers between devices  28.4 us (22%)
  waiting for transfers between devices  15.9 us (12%)
  local copies, waits for them, and re-layouts  3.56 us (3%)
  matrix products  2.26 us (2%)
  between operations  1.71 us (1%)
    psum x3, blocking collectives, global_sum(): row_sum = lax.psum(values, 'gy')  27.1 us
    ppermute x6, starting transfers between devices, padded_2(): lax.ppermute(lax.slice_in_dim(block, block.shape[dim] - width, None, axis...  20.5 us
    reduce_sum x2, other arithmetic, on_device(): curvature = global_sum(jnp.sum(direction * image, axis=(1, 2, 3)))  19.2 us
    psum x3, blocking collectives, global_sum(): return lax.psum(row_sum, 'gz')  18.1 us
    ppermute x6, waiting for transfers between devices, padded_2(): lax.ppermute(lax.slice_in_dim(block, 0, width, axis=dim), axis, backward)  15.4 us
    ppermute x6, starting transfers between devices, padded_2(): lax.ppermute(lax.slice_in_dim(block, 0, width, axis=dim), axis, backward)  7.93 us
    concatenate x5, other arithmetic, padded_2(): block = jnp.concatenate([low, block, high], axis=dim)  5.62 us
    sub x1, other arithmetic, on_device(): residual = residual - alpha * image  3.39 us
  transfers between devices with their start and end apart: 12, of which 5 were waited for; matrix products, arithmetic and copies ran while one was open for 5% of the time, Pallas kernels for 0%

commit v1 on v0

--- a/solution.py
+++ b/solution.py
@@ -59,7 +59,8 @@
 
 
 def global_sum(values):
-    row_sum = lax.psum(values, "gy")
+    terms = lax.all_gather(values, "gy")
+    row_sum = jnp.sum(terms, axis=0)
     return lax.psum(row_sum, "gz")
 
 

time: 132 us -> 136 us (1.030)
  local copies, waits for them, and re-layouts: 3.56 us -> 5.44 us
  blocking collectives: 45.2 us -> 46.6 us
    psum x3 -> x0, blocking collectives: 27.1 us -> none  [global_sum(): row_sum = lax.psum(values, 'gy')]
    unnamed x0 -> x3, blocking collectives: none -> 27 us
    unnamed x28 -> x39, local copies, waits for them, and re-layouts: 2.09 us -> 3.64 us
    psum x3, blocking collectives: 18.1 us -> 19.6 us  [global_sum(): return lax.psum(row_sum, 'gz')]
  transfers between devices with their start and end apart: 12 -> 12, of which waited for: 5 -> 6; matrix products, arithmetic and copies ran while one was open for 5% -> 5% of each run, Pallas kernels for 0% -> 0%
where the time goes in v1:
time: 136 us
  blocking collectives  46.6 us (34%)
  other arithmetic  34.3 us (25%)
  starting transfers between devices  28.2 us (21%)
  waiting for transfers between devices  16.5 us (12%)
  local copies, waits for them, and re-layouts  5.44 us (4%)
  between operations  2.43 us (2%)
  matrix products  2.26 us (2%)
    unnamed x3, blocking collectives  27 us
    ppermute x6, starting transfers between devices, padded_2(): lax.ppermute(lax.slice_in_dim(block, block.shape[dim] - width, None, axis...  20.2 us
    psum x3, blocking collectives, global_sum(): return lax.psum(row_sum, 'gz')  19.6 us
    reduce_sum x2, other arithmetic, on_device(): curvature = global_sum(jnp.sum(direction * image, axis=(1, 2, 3)))  19.1 us
    ppermute x6, waiting for transfers between devices, padded_2(): lax.ppermute(lax.slice_in_dim(block, 0, width, axis=dim), axis, backward)  15.3 us
    ppermute x6, starting transfers between devices, padded_2(): lax.ppermute(lax.slice_in_dim(block, 0, width, axis=dim), axis, backward)  7.93 us
    concatenate x5, other arithmetic, padded_2(): block = jnp.concatenate([low, block, high], axis=dim)  5.6 us
    unnamed x39, local copies, waits for them, and re-layouts  3.64 us
  transfers between devices with their start and end apart: 12, of which 6 were waited for; matrix products, arithmetic and copies ran while one was open for 5% of the time, Pallas kernels for 0%

profile of v1, /device:TPU:0, one launch (start us, length us, event | category | flops | bytes accessed | tf_op | source)
XLA Modules:
  0.0 135.7 jit_solution(16838504016877632698)
XLA Ops:
  0.6 0.0 copy-start
  0.6 0.0 copy-start.13
  0.7 0.8 select_reduce_fusion
  1.5 0.1 copy.32
  1.6 2.4 %collective-permute-start = (f32[1,16,256]{1,2,0:T(8,128)S(1)}, f32[1,16,256]{1,2,0:T(8,128)S(1)}, u32[]{:S(2)}, u32[]{:S(2)}) collective-permute-start(f32[1,16,256]{1,2,0:T(8,128)S(1)} %get-tuple-element.54), channel_id=1, source_target_pairs={{0,4},{4,8},{8,12},{1,5},{5,9},{9,13},{2,6},{6,10},{10,14},{3,7},{... | collective-permute-start | bytes 49160 | tf_op jit(solution)/shard_map/ppermute | solution.py:23
  4.0 1.3 collective-permute-start.1
  5.3 0.9 copy_bitcast_fusion.1
  6.3 1.1 multiply_reduce_fusion.2
  7.3 0.1 copy_bitcast_fusion
  7.4 0.0 copy-start.4
  7.4 1.0 copy-done.4
  8.4 5.1 %collective-permute-start.4 = (f32[8,1,16,256]{3,2,1,0:T(8,128)S(1)}, f32[8,1,16,256]{3,2,1,0:T(8,128)S(1)}, u32[]{:S(2)}, u32[]{:S(2)}) collective-permute-start(f32[8,1,16,256]{3,2,1,0:T(8,128)S(1)} %get-tuple-element.19), channel_id=1, source_target_pairs={{0,4},{4,8},{8,12},{1,5},{5,9},{9,13},{2,6},{6,10},{10,14},{3,7},{... | collective-permute-start | bytes 393224 | tf_op jit(solution)/shard_map/ppermute | solution.py:23
  13.6 1.3 collective-permute-start.5
  14.9 0.2 select_reduce_fusion.1
  15.1 0.1 copy.33
  15.8 0.6 dynamic-slice
  17.1 0.2 dynamic-update-slice
  17.3 0.1 copy.34
  17.4 0.1 copy.35
  17.5 3.5 %collective-permute-start.2 = (f32[10,1,256]{2,1,0:T(1,128)S(1)}, f32[10,1,256]{2,1,0:T(1,128)S(1)}, u32[]{:S(2)}, u32[]{:S(2)}) collective-permute-start(f32[10,1,256]{2,1,0:T(1,128)S(1)} %get-tuple-element.46), channel_id=1, source_target_pairs={{0,1},{1,2},{2,3},{4,5},{5,6},{6,7},{8,9},{9,10},{10,11},{12,13},{... | collective-permute-start | bytes 30728 | tf_op jit(solution)/shard_map/ppermute | solution.py:23
  21.0 1.3 collective-permute-start.3
  22.3 0.7 fusion.153
  23.0 3.5 %collective-permute-done.3 = f32[10,1,256]{2,1,0:T(1,128)S(1)} collective-permute-done((f32[10,1,256]{2,1,0:T(1,128)S(1)}, f32[10,1,256]{2,1,0:T(1,128)S(1)}, u32[]{:S(2)}, u32[]{:S(2)}) %collective-permute-start.3) | collective-permute-done | bytes 10272 | tf_op jit(solution)/shard_map/ppermute | solution.py:26
  26.5 0.2 select_maximum_fusion.6
  26.8 1.5 %fusion.157 = (f32[8,16,256]{2,1,0:T(8,128)S(1)}, f32[8,16,256]{2,1,0:T(8,128)S(1)}, f32[8,16,256]{2,1,0:T(8,128)S(1)}, f32[8,16,256]{2,1,0:T(8,128)S(1)}, f32[8...) fusion(f32[10,18,258]{2,1,0:T(8,128)S(1)} %select_maximum_fusio, ...), kind=kLoop, calls=%fused_computation.268 | loop fusion | flops 1179648 | bytes 4734976 | tf_op jit(solution)/shard_map/mul | solution.py:52
  28.4 0.1 constant_dynamic-update-slice_fusion.1
  28.5 0.1 fusion.160
  28.6 3.5 %collective-permute-start.6 = (f32[8,10,1,256]{3,2,1,0:T(1,128)S(1)}, f32[8,10,1,256]{3,2,1,0:T(1,128)S(1)}, u32[]{:S(2)}, u32[]{:S(2)}) collective-permute-start(f32[8,10,1,256]{3,2,1,0:T(1,128)S(1)} %get-tuple-element.14), channel_id=1, source_target_pairs={{0,1},{1,2},{2,3},{4,5},{5,6},{6,7},{8,9},{9,10},{10,11},{12,13},{... | collective-permute-start | bytes 245768 | tf_op jit(solution)/shard_map/ppermute | solution.py:23
  32.1 1.3 collective-permute-start.7
  33.4 0.9 fusion.156
  34.4 0.6 collective-permute-done.6
  34.9 4.1 %collective-permute-done.7 = f32[8,10,1,256]{3,2,1,0:T(1,128)S(1)} collective-permute-done((f32[8,10,1,256]{3,2,1,0:T(1,128)S(1)}, f32[8,10,1,256]{3,2,1,0:T(1,128)S(1)}, u32[]{:S(2)}, u32[]{:S(2)}) %collective-permute-start.7) | collective-permute-done | bytes 81952 | tf_op jit(solution)/shard_map/ppermute | solution.py:26
  39.0 1.5 %select_maximum_fusion.4 = f32[8,10,18,258]{3,2,1,0:T(8,128)S(1)} fusion(f32[8,10,1,256]{3,2,1,0:T(1,128)S(1)} %collective-permute-done.7, f32[8,10,16,256]{3,2,1,0:T(8,128)S(1)} %constant_dynamic-update-slice_fusion, f32[8,10,1,256]{3,2,1,0:T(1,128)S(1)} %collective-permute-done.6), kind=kLoop, calls=%fused_computation.6 | loop fusion | flops 2972160 | bytes 2960640 | tf_op jit(solution)/shard_map/concatenate | solution.py:27
  40.6 0.0 copy-start.5
  40.6 9.7 %multiply_reduce_fusion.1 = (f32[8]{0:T(128)S(1)}, f32[8,8,16,256]{3,2,1,0:T(8,128)S(1)}) fusion(f32[8,8,16,256]{3,2,1,0:T(8,128)} %copy-done.4, f32[8,10,18,258]{3,2,1,0:T(8,128)S(1)} %select_maximum_fusion.4, f32[8,16,256]{2,1,0:T(8,128)} %get-tuple-element.37, f32[8,10,1,256]{3,2,1,0:T(1,128)} %copy-done.10, f32[8,10,16,256]{3,2,1,0:T(8,128)} %copy-done.3, ...), kind=kLoop, calls=%fused_computation.198 | loop fusion | flops 23592952 | bytes 27164740 | tf_op jit(solution)/shard_map/reduce_sum | solution.py:97
  50.3 0.2 dynamic-update-slice.1
  50.5 9.9 %all-reduce.7 = (f32[32]{0:T(128)S(1)}, f32[32]{0:T(128)S(1)}) all-reduce(f32[32]{0:T(128)S(1)} %dynamic-update-slice, f32[32]{0:T(128)S(1)} %dynamic-update-slice.1), channel_id=2, replica_groups=mesh['sample'=2,'gz'=4,'gy'=4] {'gy'}, use_global_device_ids=true, to_apply=%add.3 | all-reduce | flops 64 | bytes 512
  60.5 0.1 reshape.85
  60.6 0.1 reshape.86
  60.7 7.0 %all-reduce.8 = (f32[8]{0:T(128)S(1)}, f32[8]{0:T(128)S(1)}) all-reduce(f32[8]{0:T(128)S(1)} %reduce_sum.91, f32[8]{0:T(128)S(1)} %reduce_sum.95), channel_id=1, replica_groups=mesh['sample'=2,'gz'=4,'gy'=4] {'gz'}, use_global_device_ids=true, to_apply=%region_2.3 | all-reduce | flops 16 | bytes 128 | tf_op jit(solution)/shard_map/psum | solution.py:64
  67.7 1.2 convolution_bitcast_fusion
  68.9 1.0 copy-done.2
  69.8 0.3 fusion.40
  70.1 0.2 dynamic-update-slice.2
  70.4 8.8 %all-reduce.5 = f32[32]{0:T(128)S(1)} all-reduce(f32[32]{0:T(128)S(1)} %dynamic-update-slice.2), channel_id=4, replica_groups=mesh['sample'=2,'gz'=4,'gy'=4] {'gy'}, use_global_device_ids=true, to_apply=%add.5 | all-reduce | flops 32 | bytes 256
  79.1 0.1 reshape.87
  79.3 5.8 %psum.30 = f32[8]{0:T(128)S(1)} all-reduce(f32[8]{0:T(128)S(1)} %reduce_sum.97), channel_id=1, replica_groups=mesh['sample'=2,'gz'=4,'gy'=4] {'gz'}, use_global_device_ids=true, to_apply=%region_10.11 | all-reduce | flops 8 | bytes 64 | tf_op jit(solution)/shard_map/psum | solution.py:64
  85.0 1.5 %bitcast_add_fusion = f32[8,8,16,256]{3,2,1,0:T(8,128)S(1)} fusion(f32[8,8,2,2,8,128]{5,4,3,2,1,0:T(8,128)} %copy-done.2, f32[8]{0:T(128)S(1)} %div.10, f32[8,8,16,2,128]{4,2,3,1,0:T(8,128)S(1)} %get-tuple-element.58), kind=kLoop, calls=%fused_computation.59 | loop fusion | flops 524288 | bytes 3145760 | tf_op jit(solution)/shard_map/add | solution.py:103
  86.6 2.3 %collective-permute-start.8 = (f32[8,1,16,256]{3,2,1,0:T(8,128)S(1)}, f32[8,1,16,256]{3,2,1,0:T(8,128)S(1)}, u32[]{:S(2)}, u32[]{:S(2)}) collective-permute-start(f32[8,1,16,256]{3,2,1,0:T(8,128)S(1)} %get-tuple-element.16), channel_id=1, source_target_pairs={{0,4},{4,8},{8,12},{1,5},{5,9},{9,13},{2,6},{6,10},{10,14},{3,7},{... | collective-permute-start | bytes 393224 | tf_op jit(solution)/shard_map/ppermute | solution.py:23
  88.9 1.3 collective-permute-start.9
  90.2 3.4 %collective-permute-done.9 = f32[8,1,16,256]{3,2,1,0:T(8,128)S(1)} collective-permute-done((f32[8,1,16,256]{3,2,1,0:T(8,128)S(1)}, f32[8,1,16,256]{3,2,1,0:T(8,128)S(1)}, u32[]{:S(2)}, u32[]{:S(2)}) %collective-permute-start.9) | collective-permute-done | bytes 131104 | tf_op jit(solution)/shard_map/ppermute | solution.py:26
  93.6 0.1 pad_maximum_fusion.12
  93.7 3.5 %collective-permute-start.10 = (f32[8,10,1,256]{3,2,1,0:T(1,128)S(1)}, f32[8,10,1,256]{3,2,1,0:T(1,128)S(1)}, u32[]{:S(2)}, u32[]{:S(2)}) collective-permute-start(f32[8,10,1,256]{3,2,1,0:T(1,128)S(1)} %get-tuple-element.12), channel_id=1, source_target_pairs={{0,1},{1,2},{2,3},{4,5},{5,6},{6,7},{8,9},{9,10},{10,11},{12,13},{... | collective-permute-start | bytes 245768 | tf_op jit(solution)/shard_map/ppermute | solution.py:23
  97.2 1.5 %collective-permute-start.11 = (f32[8,10,1,256]{3,2,1,0:T(1,128)S(1)}, f32[8,10,1,256]{3,2,1,0:T(1,128)S(1)}, u32[]{:S(2)}, u32[]{:S(2)}) collective-permute-start(f32[8,10,1,256]{3,2,1,0:T(1,128)S(1)} %get-tuple-element.13), channel_id=1, source_target_pairs={{1,0},{2,1},{3,2},{5,4},{6,5},{7,6},{9,8},{10,9},{11,10},{13,12},{... | collective-permute-start | bytes 245768 | tf_op jit(solution)/shard_map/ppermute | solution.py:26
  98.7 0.6 collective-permute-done.10
  99.2 4.3 %collective-permute-done.11 = f32[8,10,1,256]{3,2,1,0:T(1,128)S(1)} collective-permute-done((f32[8,10,1,256]{3,2,1,0:T(1,128)S(1)}, f32[8,10,1,256]{3,2,1,0:T(1,128)S(1)}, u32[]{:S(2)}, u32[]{:S(2)}) %collective-permute-start.11) | collective-permute-done | bytes 81952 | tf_op jit(solution)/shard_map/ppermute | solution.py:26
  103.5 2.3 %maximum_maximum_fusion = (f32[8,10,17,256]{3,2,1,0:T(8,128)}, f32[8,10,17,256]{3,2,1,0:T(8,128)}) fusion(f32[8,1,16,256]{3,2,1,0:T(8,128)S(1)} %collective-permute-done.9, f32[8,8,16,256]{3,2,1,0:T(8,128)S(1)} %bitcast_add_fusion, f32[8,1,16,256]{3,2,1,0:T(8,128)S(1)} %collective-permute-done.8, f32[8,10,1,256]{3,2,1,0:T(1,128)S(1)} %collective-permute-done.10, ...), kind=kLoop, calls=%fused_computation.17 | loop fusion | flops 2088960 | bytes 4259840 | tf_op jit(solution)/shard_map/concatenate | solution.py:27
  105.9 1.5 %select_maximum_fusion = f32[8,10,18,258]{3,2,1,0:T(8,128)S(1)} fusion(f32[8,10,1,256]{3,2,1,0:T(1,128)S(1)} %collective-permute-done.11, f32[8,10,1,256]{3,2,1,0:T(1,128)S(1)} %collective-permute-done.10, f32[8,1,16,256]{3,2,1,0:T(8,128)S(1)} %collective-permute-done.9, f32[8,8,16,256]{3,2,1,0:T(8,128)S(1)} %bitcast_add_fusion, ...), kind=kLoop, calls=%fused_computation.2 | loop fusion | flops 4458240 | bytes 2960640 | tf_op jit(solution)/shard_map/concatenate | solution.py:27
  107.4 9.4 %multiply_reduce_fusion = (f32[8]{0:T(128)S(1)}, f32[8,8,16,256]{3,2,1,0:T(8,128)}) fusion(f32[8,8,16,256]{3,2,1,0:T(8,128)S(1)} %bitcast_add_fusion, f32[8,10,18,258]{3,2,1,0:T(8,128)S(1)} %select_maximum_fusion, f32[8,16,256]{2,1,0:T(8,128)} %get-tuple-element.37, f32[8,10,17,256]{3,2,1,0:T(8,128)} %get-tuple-element.11, ...), kind=kLoop, calls=%fused_computation.196 | loop fusion | flops 22020088 | bytes 30933060 | tf_op jit(solution)/shard_map/reduce_sum | solution.py:97
  116.8 0.2 dynamic-update-slice.3
  117.0 8.3 %all-reduce.6 = f32[32]{0:T(128)S(1)} all-reduce(f32[32]{0:T(128)S(1)} %dynamic-update-slice.3), channel_id=5, replica_groups=mesh['sample'=2,'gz'=4,'gy'=4] {'gy'}, use_global_device_ids=true, to_apply=%add.6 | all-reduce | flops 32 | bytes 256
  125.3 0.1 reshape.88
  125.5 6.9 %psum.31 = f32[8]{0:T(128)S(1)} all-reduce(f32[8]{0:T(128)S(1)} %reduce_sum.99), channel_id=1, replica_groups=mesh['sample'=2,'gz'=4,'gy'=4] {'gz'}, use_global_device_ids=true, to_apply=%region_13.14 | all-reduce | flops 8 | bytes 64 | tf_op jit(solution)/shard_map/psum | solution.py:64
  132.3 3.4 %multiply_subtract_fusion = (f32[8,8,16,256]{3,2,1,0:T(8,128)}, f32[8,8,16,256]{3,2,1,0:T(8,128)}) fusion(f32[8,8,16,256]{3,2,1,0:T(8,128)} %get-tuple-element.7, f32[8,8,16,256]{3,2,1,0:T(8,128)} %copy-done.1, f32[8]{0:T(128)S(1)} %div.11, f32[8,16,256]{2,1,0:T(8,128)S(1)} %copy-done.5, f32[8]{0:T(128)S(1)} %div.9, ...), kind=kLoop, calls=%fused_computation.194 | loop fusion | flops 1835008 | bytes 6422592 | tf_op jit(solution)/shard_map/sub | solution.py:100
  (48 shorter events, 0.3 us)
Async XLA Ops:
  0.6 5.6 %copy-start = (f32[8,128,128]{2,1,0:T(8,128)S(1)}, f32[8,128,128]{2,1,0:T(8,128)}, u32[]{:S(2)}) copy-start(f32[8,128,128]{2,1,0:T(8,128)} %param.13) | copy-start | bytes 1572868
  0.6 15.2 %copy-start.13 = (u32[32]{0:T(128)S(1)}, u32[32]{0:T(128)}, u32[]{:S(2)}) copy-start(u32[32]{0:T(128)} %constant.20) | copy-start | bytes 388
  0.7 14.2 %copy-start.12 = (s32[8]{0:T(128)S(1)}, s32[8]{0:T(128)}, u32[]{:S(2)}) copy-start(s32[8]{0:T(128)} %param.10) | copy-start | bytes 100
  0.7 14.2 %copy-start.11 = (f32[16]{0:T(128)S(1)}, f32[16]{0:T(128)}, u32[]{:S(2)}) copy-start(f32[16]{0:T(128)} %param.11) | copy-start | bytes 196
  1.6 15.7 %collective-permute-start = (f32[1,16,256]{1,2,0:T(8,128)S(1)}, f32[1,16,256]{1,2,0:T(8,128)S(1)}, u32[]{:S(2)}, u32[]{:S(2)}) collective-permute-start(f32[1,16,256]{1,2,0:T(8,128)S(1)} %get-tuple-element.54), channel_id=1, source_target_pairs={{0,4},{4,8},{8,12},{1,5},{5,9},{9,13},{2,6},{6,10},{10,14},{3,7},{... | collective-permute-start | bytes 49160 | tf_op jit(solution)/shard_map/ppermute | solution.py:23
  4.0 13.3 %collective-permute-start.1 = (f32[1,16,256]{1,2,0:T(8,128)S(1)}, f32[1,16,256]{1,2,0:T(8,128)S(1)}, u32[]{:S(2)}, u32[]{:S(2)}) collective-permute-start(f32[1,16,256]{1,2,0:T(8,128)S(1)} %get-tuple-element.54), channel_id=1, source_target_pairs={{4,0},{8,4},{12,8},{5,1},{9,5},{13,9},{6,2},{10,6},{14,10},{7,3},{... | collective-permute-start | bytes 49160 | tf_op jit(solution)/shard_map/ppermute | solution.py:26
  7.4 1.0 copy-start.4
  8.4 19.9 %collective-permute-start.4 = (f32[8,1,16,256]{3,2,1,0:T(8,128)S(1)}, f32[8,1,16,256]{3,2,1,0:T(8,128)S(1)}, u32[]{:S(2)}, u32[]{:S(2)}) collective-permute-start(f32[8,1,16,256]{3,2,1,0:T(8,128)S(1)} %get-tuple-element.19), channel_id=1, source_target_pairs={{0,4},{4,8},{8,12},{1,5},{5,9},{9,13},{2,6},{6,10},{10,14},{3,7},{... | collective-permute-start | bytes 393224 | tf_op jit(solution)/shard_map/ppermute | solution.py:23
  13.6 14.9 %collective-permute-start.5 = (f32[8,1,16,256]{3,2,1,0:T(8,128)S(1)}, f32[8,1,16,256]{3,2,1,0:T(8,128)S(1)}, u32[]{:S(2)}, u32[]{:S(2)}) collective-permute-start(f32[8,1,16,256]{3,2,1,0:T(8,128)S(1)} %get-tuple-element.18), channel_id=1, source_target_pairs={{4,0},{8,4},{12,8},{5,1},{9,5},{13,9},{6,2},{10,6},{14,10},{7,3},{... | collective-permute-start | bytes 393224 | tf_op jit(solution)/shard_map/ppermute | solution.py:26
  17.5 5.5 %collective-permute-start.2 = (f32[10,1,256]{2,1,0:T(1,128)S(1)}, f32[10,1,256]{2,1,0:T(1,128)S(1)}, u32[]{:S(2)}, u32[]{:S(2)}) collective-permute-start(f32[10,1,256]{2,1,0:T(1,128)S(1)} %get-tuple-element.46), channel_id=1, source_target_pairs={{0,1},{1,2},{2,3},{4,5},{5,6},{6,7},{8,9},{9,10},{10,11},{12,13},{... | collective-permute-start | bytes 30728 | tf_op jit(solution)/shard_map/ppermute | solution.py:23
  21.0 5.6 %collective-permute-start.3 = (f32[10,1,256]{2,1,0:T(1,128)S(1)}, f32[10,1,256]{2,1,0:T(1,128)S(1)}, u32[]{:S(2)}, u32[]{:S(2)}) collective-permute-start(f32[10,1,256]{2,1,0:T(1,128)S(1)} %get-tuple-element.47), channel_id=1, source_target_pairs={{1,0},{2,1},{3,2},{5,4},{6,5},{7,6},{9,8},{10,9},{11,10},{13,12},{... | collective-permute-start | bytes 30728 | tf_op jit(solution)/shard_map/ppermute | solution.py:26
  28.3 12.3 %copy-start.6 = (f32[8,16,256]{2,1,0:T(8,128)}, f32[8,16,256]{2,1,0:T(8,128)S(1)}, u32[]{:S(2)}) copy-start(f32[8,16,256]{2,1,0:T(8,128)S(1)} %get-tuple-element.25) | copy-start | bytes 393220
  28.3 12.3 %copy-start.7 = (f32[8,16,256]{2,1,0:T(8,128)}, f32[8,16,256]{2,1,0:T(8,128)S(1)}, u32[]{:S(2)}) copy-start(f32[8,16,256]{2,1,0:T(8,128)S(1)} %get-tuple-element.26) | copy-start | bytes 393220
  28.3 12.2 %copy-start.8 = (f32[8,1,16,256]{3,2,1,0:T(8,128)}, f32[8,1,16,256]{3,2,1,0:T(8,128)S(1)}, u32[]{:S(2)}) copy-start(f32[8,1,16,256]{3,2,1,0:T(8,128)S(1)} %collective-permute-done.4) | copy-start | bytes 393220
  28.5 12.1 %copy-start.9 = (f32[8,1,16,256]{3,2,1,0:T(8,128)}, f32[8,1,16,256]{3,2,1,0:T(8,128)S(1)}, u32[]{:S(2)}) copy-start(f32[8,1,16,256]{3,2,1,0:T(8,128)S(1)} %collective-permute-done.5) | copy-start | bytes 393220
  28.5 12.0 %copy-start.3 = (f32[8,10,16,256]{3,2,1,0:T(8,128)}, f32[8,10,16,256]{3,2,1,0:T(8,128)S(1)}, u32[]{:S(2)}) copy-start(f32[8,10,16,256]{3,2,1,0:T(8,128)S(1)} %constant_dynamic-update-slice_fusion) | copy-start | bytes 3932164
  28.6 6.3 %collective-permute-start.6 = (f32[8,10,1,256]{3,2,1,0:T(1,128)S(1)}, f32[8,10,1,256]{3,2,1,0:T(1,128)S(1)}, u32[]{:S(2)}, u32[]{:S(2)}) collective-permute-start(f32[8,10,1,256]{3,2,1,0:T(1,128)S(1)} %get-tuple-element.14), channel_id=1, source_target_pairs={{0,1},{1,2},{2,3},{4,5},{5,6},{6,7},{8,9},{9,10},{10,11},{12,13},{... | collective-permute-start | bytes 245768 | tf_op jit(solution)/shard_map/ppermute | solution.py:23
  32.1 6.9 %collective-permute-start.7 = (f32[8,10,1,256]{3,2,1,0:T(1,128)S(1)}, f32[8,10,1,256]{3,2,1,0:T(1,128)S(1)}, u32[]{:S(2)}, u32[]{:S(2)}) collective-permute-start(f32[8,10,1,256]{3,2,1,0:T(1,128)S(1)} %get-tuple-element.15), channel_id=1, source_target_pairs={{1,0},{2,1},{3,2},{5,4},{6,5},{7,6},{9,8},{10,9},{11,10},{13,12},{... | collective-permute-start | bytes 245768 | tf_op jit(solution)/shard_map/ppermute | solution.py:26
  39.0 1.5 %copy-start.10 = (f32[8,10,1,256]{3,2,1,0:T(1,128)}, f32[8,10,1,256]{3,2,1,0:T(1,128)S(1)}, u32[]{:S(2)}) copy-start(f32[8,10,1,256]{3,2,1,0:T(1,128)S(1)} %collective-permute-done.7) | copy-start | bytes 245764
  40.6 27.1 %copy-start.5 = (f32[8,16,256]{2,1,0:T(8,128)S(1)}, f32[8,16,256]{2,1,0:T(8,128)}, u32[]{:S(2)}) copy-start(f32[8,16,256]{2,1,0:T(8,128)} %param.7) | copy-start | bytes 393220
  50.3 34.7 %copy-start.1 = (f32[8,8,16,256]{3,2,1,0:T(8,128)}, f32[8,8,16,256]{3,2,1,0:T(8,128)S(1)}, u32[]{:S(2)}) copy-start(f32[8,8,16,256]{3,2,1,0:T(8,128)S(1)} %get-tuple-element.9) | copy-start | bytes 3145732
  68.8 1.0 copy-start.2
  86.6 3.6 %collective-permute-start.8 = (f32[8,1,16,256]{3,2,1,0:T(8,128)S(1)}, f32[8,1,16,256]{3,2,1,0:T(8,128)S(1)}, u32[]{:S(2)}, u32[]{:S(2)}) collective-permute-start(f32[8,1,16,256]{3,2,1,0:T(8,128)S(1)} %get-tuple-element.16), channel_id=1, source_target_pairs={{0,4},{4,8},{8,12},{1,5},{5,9},{9,13},{2,6},{6,10},{10,14},{3,7},{... | collective-permute-start | bytes 393224 | tf_op jit(solution)/shard_map/ppermute | solution.py:23
  88.9 4.7 %collective-permute-start.9 = (f32[8,1,16,256]{3,2,1,0:T(8,128)S(1)}, f32[8,1,16,256]{3,2,1,0:T(8,128)S(1)}, u32[]{:S(2)}, u32[]{:S(2)}) collective-permute-start(f32[8,1,16,256]{3,2,1,0:T(8,128)S(1)} %get-tuple-element.17), channel_id=1, source_target_pairs={{4,0},{8,4},{12,8},{5,1},{9,5},{13,9},{6,2},{10,6},{14,10},{7,3},{... | collective-permute-start | bytes 393224 | tf_op jit(solution)/shard_map/ppermute | solution.py:26
  93.7 5.5 %collective-permute-start.10 = (f32[8,10,1,256]{3,2,1,0:T(1,128)S(1)}, f32[8,10,1,256]{3,2,1,0:T(1,128)S(1)}, u32[]{:S(2)}, u32[]{:S(2)}) collective-permute-start(f32[8,10,1,256]{3,2,1,0:T(1,128)S(1)} %get-tuple-element.12), channel_id=1, source_target_pairs={{0,1},{1,2},{2,3},{4,5},{5,6},{6,7},{8,9},{9,10},{10,11},{12,13},{... | collective-permute-start | bytes 245768 | tf_op jit(solution)/shard_map/ppermute | solution.py:23
  97.2 6.3 %collective-permute-start.11 = (f32[8,10,1,256]{3,2,1,0:T(1,128)S(1)}, f32[8,10,1,256]{3,2,1,0:T(1,128)S(1)}, u32[]{:S(2)}, u32[]{:S(2)}) collective-permute-start(f32[8,10,1,256]{3,2,1,0:T(1,128)S(1)} %get-tuple-element.13), channel_id=1, source_target_pairs={{1,0},{2,1},{3,2},{5,4},{6,5},{7,6},{9,8},{10,9},{11,10},{13,12},{... | collective-permute-start | bytes 245768 | tf_op jit(solution)/shard_map/ppermute | solution.py:26
